TPU v7x, 32 devices: a whole 2x2x4 slice. The times are simulated.
32 devices in a mesh: chain: 4 (over y, core), cols: 8 (over z, x).
Axes of the slice: x: 2, y: 2, z: 4, core: 2. Of those that a mesh axis runs over, the one named last changes fastest.
Arguments:
- factor: float32 [4608, 4608], P(('chain', 'cols')), may hold values from -2 to 2, as said below
- right_side: float32 [4608, 1024], P('chain', 'cols'), may hold values from -6 to 6
- occ_order: int32 [16], replicated, may hold values from 0 to 15, each once
- cabs_order: int32 [64], replicated, may hold values from 0 to 63, each once
Outputs:
- fitted: float32 [16, 64, 4608], P('cols', None, 'chain')
Inputs may be any that keep to these rules, and one draw needn't show every extreme that they name: factor is lower triangular: zero above the diagonal, its diagonal between 1 and 2.
All inputs are finite; a program needn't handle non-finite values.
Results may differ from a plain program's by a relative error of at most 0.00017.
Values sent between devices are 32-bit elements; how exact they have to be, the bound alone decides.
A program may use at most 128 MiB of HBM per device.

v0:
```python
import jax
import jax.numpy as jnp
from jax import lax
from jax.sharding import PartitionSpec as P


def from_root(value, axis, source):
    kept = jnp.where(lax.axis_index(axis) == source, value, 0).astype(value.dtype)
    return lax.psum(kept, axis)


def product(left, right):
    return jnp.dot(left, right, precision=lax.Precision.HIGHEST, preferred_element_type=jnp.float32)


def per_device(factor, right_side, occ_order, cabs_order):
    chain_size = lax.axis_size("chain")
    position = lax.axis_index("chain")
    factor_row = lax.all_gather(factor, "cols", axis=0, tiled=True)
    aux_rows = factor_row.shape[0]
    diag_block = lax.dynamic_slice_in_dim(factor_row, position * aux_rows, aux_rows, 1)
    identity = jnp.eye(aux_rows, dtype=jnp.float32)
    inverse = jax.scipy.linalg.solve_triangular(diag_block, identity, lower=True)

    def settle(residual):
        return product(inverse, residual)

    def blank(residual):
        return jnp.zeros_like(residual)

    residual = right_side
    solution = jnp.zeros_like(right_side)
    for section in range(chain_size):
        solved = lax.cond(position == section, settle, blank, residual)
        solution = solution + solved
        if section + 1 < chain_size:
            arrived = from_root(solved, "chain", section)
            coupling = factor_row[:, section * aux_rows : (section + 1) * aux_rows]

            def lower_block(current, arrived=arrived, coupling=coupling):
                return current - product(coupling, arrived)

            def keep_block(current):
                return current

            residual = lax.cond(position > section, lower_block, keep_block, residual)
    occ_total = occ_order.shape[0]
    cabs_local = right_side.shape[1] // occ_total
    cols_size = lax.axis_size("cols")
    occ_local = occ_total // cols_size
    grid = solution.reshape(aux_rows, cabs_local, occ_total)
    grid = jnp.take(grid, occ_order, axis=2)
    grid = grid.reshape(aux_rows, cabs_local, cols_size, occ_local)
    grid = jnp.transpose(grid, (2, 3, 1, 0))
    moved = jnp.take(
        lax.all_to_all(grid, "cols", split_axis=0, concat_axis=2, tiled=True), cabs_order, axis=2
    )
    return moved.reshape(occ_local, moved.shape[2], aux_rows)


def solution(mesh):
    in_specs = (P(("chain", "cols"), None), P("chain", "cols"), P(), P())
    out_specs = P("cols", None, "chain")
    return jax.shard_map(
        per_device, mesh=mesh, in_specs=in_specs, out_specs=out_specs, check_vma=False
    )
```

profile of v0, /device:TPU:5, one launch (start us, length us, event | category | flops | bytes accessed | tf_op | source)
XLA Modules:
  0.0 739.5 jit_solution(7682201106156119193)
XLA Ops:
  6.5 1.1 copy.72
  7.7 0.4 iota_compare_fusion
  8.1 2.7 fusion.27
  10.8 405.7 %all-gather.2.cloned.1.call-done = f32[1152,4608]{1,0:T(8,128)} async-done(((f32[144,4608]{1,0:T(8,128)}), f32[1152,4608]{1,0:T(8,128)}) %all-gather.2.cloned.1.call-update) | async-done | bytes 21233680 | tf_op jit(solution)/shard_map/all_gather | solution.py:19
  416.6 5.2 dynamic-slice_select_fusion
  421.8 25.2 %while.1 = (s32[]{:T(128)}, f32[1152,1152]{1,0:T(8,128)}, s32[9,2]{0,1:T(2,128)S(1)}, f32[9,128,128]{2,1,0:T(8,128)S(1)}, s32[]{:T(128)}) while((s32[]{:T(128)}, f32[1152,1152]{1,0:T(8,128)}, s32[9,2]{0,1:T(2,128)S(1)}, f32[9,128,128]{2,1,0:T(8,128)S(1)}, s32[]{:T(128)}) %tuple.105), condition=%wide.while_cond, body=%wide.while_body.sunk | while | flops 2 | bytes 131181 | solution.py:23
  421.8 0.5 fusion.82
  422.4 2.2 bitcast_dynamic-update-slice_fusion.2
  424.6 0.5 fusion.82
  425.2 2.2 bitcast_dynamic-update-slice_fusion.2
  427.5 0.5 fusion.82
  428.0 2.2 bitcast_dynamic-update-slice_fusion.2
  430.3 0.5 fusion.82
  430.8 2.2 bitcast_dynamic-update-slice_fusion.2
  433.1 0.5 fusion.82
  433.6 2.2 bitcast_dynamic-update-slice_fusion.2
  435.9 0.5 fusion.82
  436.4 2.2 bitcast_dynamic-update-slice_fusion.2
  438.7 0.5 fusion.82
  439.2 2.2 bitcast_dynamic-update-slice_fusion.2
  441.5 0.5 fusion.82
  442.1 2.2 bitcast_dynamic-update-slice_fusion.2
  444.3 0.5 fusion.82
  444.9 2.1 bitcast_dynamic-update-slice_fusion.2
  447.0 88.9 %custom-call.4 = f32[9,128,128]{1,2,0:T(8,128)S(1)} custom-call(f32[9,128,128]{2,1,0:T(8,128)S(1)} %get-tuple-element.90), custom_call_target="InvertDiagBlocksLowerTriangular" | custom-call | tf_op jit(solution)/shard_map/jit(_solve_triangular)/triangular_solve | solution.py:23
  535.9 0.7 constant_dynamic-update-slice_fusion.25
  536.6 2.1 convolution_subtract_fusion.7
  538.7 0.9 constant_dynamic-update-slice_fusion.24
  539.6 1.7 convolution_subtract_fusion.6
  541.3 0.8 constant_dynamic-update-slice_fusion.23
  542.1 2.3 convolution_subtract_fusion.2
  544.4 0.9 constant_dynamic-update-slice_fusion.22
  545.3 2.4 convolution_subtract_fusion.5
  547.7 0.8 constant_dynamic-update-slice_fusion.21
  548.5 3.0 convolution_subtract_fusion
  551.5 0.7 constant_dynamic-update-slice_fusion.20
  552.2 3.4 convolution_subtract_fusion.1
  555.6 0.7 constant_dynamic-update-slice_fusion.19
  556.3 3.7 convolution_subtract_fusion.4
  560.0 0.7 constant_dynamic-update-slice_fusion.18
  560.7 3.9 convolution_subtract_fusion.3
  564.6 0.7 convolution_dynamic-update-slice_fusion
  565.3 2.3 copy-done
  567.9 0.9 broadcast_select_fusion.2
  568.8 35.9 %all-reduce.4.cloned.1.call-done = f32[1152,128]{1,0:T(8,128)} async-done(((f32[1152,128]{1,0:T(8,128)}), f32[1152,128]{1,0:T(8,128)}) %all-reduce.4.cloned.1.call-update) | async-done | bytes 589840 | tf_op jit(solution)/shard_map/psum | solution.py:9
  604.7 6.4 conditional.8
  604.7 6.4 fusion.2
  611.2 0.9 broadcast_select_fusion.1
  612.3 38.6 %all-reduce.6.cloned.1.call-done = f32[1152,128]{1,0:T(8,128)} async-done(((f32[1152,128]{1,0:T(8,128)}), f32[1152,128]{1,0:T(8,128)}) %all-reduce.6.cloned.1.call-update) | async-done | bytes 589840 | tf_op jit(solution)/shard_map/psum | solution.py:9
  650.9 6.4 conditional.10
  650.9 6.4 fusion.7
  657.4 0.9 broadcast_select_fusion
  659.0 39.4 %all-reduce.8.cloned.1.call-done = f32[1152,128]{1,0:T(8,128)} async-done(((f32[1152,128]{1,0:T(8,128)}), f32[1152,128]{1,0:T(8,128)}) %all-reduce.8.cloned.1.call-update) | async-done | bytes 589840 | tf_op jit(solution)/shard_map/psum | solution.py:9
  698.4 6.7 conditional.12
  698.6 6.4 fusion.12
  705.0 7.4 %conditional.13 = (f32[1152,128]{0,1:T(8,128)S(1)}) conditional(s32[]{:T(128)} %convert_element_type.48, () %tuple.55, (f32[1152,1152]{1,0:T(8,128)}, f32[1152,128]{1,0:T(8,128)S(1)}) %tuple.132), branch_computations={%region_15.16_spmd, %region_16.17_spmd} | conditional | flops 2038431744 | bytes 6488072 | solution.py:34
  705.0 7.4 %fusion.55 = f32[1152,128]{0,1:T(8,128)S(1)} fusion(f32[1152,1152]{1,0:T(8,128)} %get-tuple-element.79, f32[1152,128]{1,0:T(8,128)S(1)} %get-tuple-element.80), kind=kOutput, calls=%fused_computation.122 | convolution fusion | flops 2038431744 | bytes 6488064 | tf_op jit(solution)/shard_map/cond | solution.py:34
  712.8 0.6 gather_fusion
  713.4 0.9 select_bitcast_fusion.1
  714.3 5.5 all-to-all-start
  719.8 9.8 %all-to-all-done = f32[8,2,8,1152]{3,2,1,0:T(8,128)S(1)} async-done(((f32[8,2,8,1152]{3,2,1,0:T(8,128)}), f32[8,2,8,1152]{3,2,1,0:T(8,128)S(1)}, u32[]{:S(2)}, u32[]{:S(2)}) %all-to-all-start) | async-done | bytes 589856 | tf_op jit(solution)/shard_map/all_to_all | solution.py:56
  729.7 0.5 copy.11
  730.2 1.2 gather_fusion.1
  731.7 0.9 copy.12
  (46 shorter events, 2.9 us)
Async XLA Ops:
  6.5 410.0 %all-gather.2.cloned.1.call-start = ((), (), s32[]{:S(2)}) async-start(), calls=%async_computation.1 | async-start | bytes 23887872 | tf_op jit(solution)/shard_map/all_gather | solution.py:19
  7.6 597.1 %all-reduce.4.cloned.1.call-start = ((), (), s32[]{:S(2)}) async-start(), calls=%async_computation.2 | async-start | bytes 1179648 | tf_op jit(solution)/shard_map/psum | solution.py:9
  535.9 3.6 copy-start.1
  565.3 2.3 copy-start
  568.8 82.1 %all-reduce.6.cloned.1.call-start = ((), (), s32[]{:S(2)}) async-start(), calls=%async_computation.3 | async-start | bytes 1179648 | tf_op jit(solution)/shard_map/psum | solution.py:9
  611.1 1.0 copy-start.2
  612.1 86.2 %all-reduce.8.cloned.1.call-start = ((), (), s32[]{:S(2)}) async-start(), calls=%async_computation.4 | async-start | bytes 1179648 | tf_op jit(solution)/shard_map/psum | solution.py:9
  657.3 1.0 copy-start.3
  714.3 15.3 %all-to-all-start = ((f32[8,2,8,1152]{3,2,1,0:T(8,128)}), f32[8,2,8,1152]{3,2,1,0:T(8,128)S(1)}, u32[]{:S(2)}, u32[]{:S(2)}) async-start(f32[8,2,8,1152]{3,2,1,0:T(8,128)} %select_bitcast_fusion.1), calls=%async_computation | async-start | bytes 1179648 | tf_op jit(solution)/shard_map/all_to_all | solution.py:56
Sparse Core Ops, SparseCore 0:
  8.9 407.6 all-gather.1
  568.9 35.8 all-reduce.3
  612.2 38.5 all-reduce.5
  658.4 39.9 all-reduce.7
where the time goes:
time: 744 us; the launch traced here: 740 us
  waiting for transfers between devices  529 us (71%)
  other arithmetic  101 us (14%)
  matrix products  55.8 us (8%)
  local copies, waits for them, and re-layouts  32.7 us (4%)
  between operations  13.9 us (2%)
    all_gather x1, waiting for transfers between devices, per_device(): factor_row = lax.all_gather(factor, 'cols', axis=0, tiled=True)  406 us
    psum x3, waiting for transfers between devices, from_root(): return lax.psum(kept, axis)  114 us
    another operation x3, other arithmetic, per_device(): jax.scipy.linalg.solve_triangular(diag_block, identity, lower=True)  94.1 us
    another operation x17, matrix products, per_device(): jax.scipy.linalg.solve_triangular(diag_block, identity, lower=True)  29.2 us
    another operation x30, local copies, waits for them, and re-layouts  25.2 us
    dot_general x3, matrix products, product(): jnp.dot(left, right, precision=lax.Precision.HIGHEST, preferred_element_t...  19.2 us
  transfers between devices with their start and end apart: 5, of which 5 were waited for; matrix products, arithmetic and copies ran while one was open for 1% of the time, Pallas kernels for 0%

commit v1 on v0

--- a/solution.py
+++ b/solution.py
@@ -6,7 +6,7 @@
 
 def from_root(value, axis, source):
     kept = jnp.where(lax.axis_index(axis) == source, value, 0).astype(value.dtype)
-    return lax.psum(kept, axis)
+    return jnp.sum(lax.all_gather(kept, axis), 0)
 
 
 def product(left, right):

time: 744 us -> 728 us (0.978)
  waiting for transfers between devices: 529 us -> 504 us
    psum x3 -> x0, waiting for transfers between devices: 114 us -> none  [from_root(): return lax.psum(kept, axis)]
    all_gather x0 -> x3, waiting for transfers between devices: none -> 87 us  [from_root(): return jnp.sum(lax.all_gather(kept, axis), 0)]
    another operation x30 -> x31, local copies, waits for them, and re-layouts: 25.2 us -> 26.7 us
where the time goes in v1:
time: 728 us; the launch traced here: 724 us
  waiting for transfers between devices  504 us (69%)
  other arithmetic  106 us (15%)
  matrix products  60.4 us (8%)
  local copies, waits for them, and re-layouts  33.2 us (5%)
  between operations  13.7 us (2%)
    all_gather x1, waiting for transfers between devices, per_device(): factor_row = lax.all_gather(factor, 'cols', axis=0, tiled=True)  406 us
    another operation x3, other arithmetic, per_device(): jax.scipy.linalg.solve_triangular(diag_block, identity, lower=True)  93.8 us
    all_gather x3, waiting for transfers between devices, from_root(): return jnp.sum(lax.all_gather(kept, axis), 0)  87 us
    another operation x17, matrix products, per_device(): jax.scipy.linalg.solve_triangular(diag_block, identity, lower=True)  29.2 us
    another operation x31, local copies, waits for them, and re-layouts  26.7 us
    dot_general x3, matrix products, product(): jnp.dot(left, right, precision=lax.Precision.HIGHEST, preferred_element_t...  23.6 us
  transfers between devices with their start and end apart: 5, of which 5 were waited for; matrix products, arithmetic and copies ran while one was open for 1% of the time, Pallas kernels for 0%

profile of v1, /device:TPU:5, one launch (start us, length us, event | category | flops | bytes accessed | tf_op | source)
XLA Modules:
  0.0 724.0 jit_solution(8520998087109370749)
XLA Ops:
  6.5 0.7 all-gather.8.cloned.1.call-update
  7.7 2.7 fusion.36
  10.5 406.1 %all-gather.8.cloned.1.call-done = f32[1152,4608]{1,0:T(8,128)} async-done(((f32[144,4608]{1,0:T(8,128)}), f32[1152,4608]{1,0:T(8,128)}) %all-gather.8.cloned.1.call-update) | async-done | bytes 21233680 | tf_op jit(solution)/shard_map/all_gather | solution.py:19
  416.6 5.2 dynamic-slice_select_fusion
  421.8 26.5 %while.1 = (s32[]{:T(128)}, f32[1152,1152]{1,0:T(8,128)}, s32[9,2]{0,1:T(2,128)S(1)}, f32[9,128,128]{2,1,0:T(8,128)S(1)}, s32[]{:T(128)}) while((s32[]{:T(128)}, f32[1152,1152]{1,0:T(8,128)}, s32[9,2]{0,1:T(2,128)S(1)}, f32[9,128,128]{2,1,0:T(8,128)S(1)}, s32[]{:T(128)}) %tuple.114), condition=%wide.while_cond, body=%wide.while_body.sunk | while | flops 2 | bytes 131181 | solution.py:23
  422.4 2.3 bitcast_dynamic-update-slice_fusion.2
  424.8 0.6 fusion.91
  425.4 2.3 bitcast_dynamic-update-slice_fusion.2
  427.7 0.6 fusion.91
  428.3 2.3 bitcast_dynamic-update-slice_fusion.2
  430.7 0.6 fusion.91
  431.3 2.3 bitcast_dynamic-update-slice_fusion.2
  433.6 0.6 fusion.91
  434.2 2.3 bitcast_dynamic-update-slice_fusion.2
  436.6 0.6 fusion.91
  437.2 2.3 bitcast_dynamic-update-slice_fusion.2
  439.5 0.6 fusion.91
  440.1 2.3 bitcast_dynamic-update-slice_fusion.2
  442.5 0.6 fusion.91
  443.1 2.3 bitcast_dynamic-update-slice_fusion.2
  445.4 0.6 fusion.91
  446.0 2.2 bitcast_dynamic-update-slice_fusion.2
  448.3 88.6 %custom-call.4 = f32[9,128,128]{1,2,0:T(8,128)S(1)} custom-call(f32[9,128,128]{2,1,0:T(8,128)S(1)} %get-tuple-element.96), custom_call_target="InvertDiagBlocksLowerTriangular" | custom-call | tf_op jit(solution)/shard_map/jit(_solve_triangular)/triangular_solve | solution.py:23
  536.9 0.7 constant_dynamic-update-slice_fusion.25
  537.5 2.1 convolution_subtract_fusion.7
  539.6 0.8 constant_dynamic-update-slice_fusion.24
  540.5 1.7 convolution_subtract_fusion.6
  542.2 0.8 constant_dynamic-update-slice_fusion.23
  543.0 2.3 convolution_subtract_fusion.2
  545.3 0.9 constant_dynamic-update-slice_fusion.22
  546.2 2.4 convolution_subtract_fusion.5
  548.6 0.8 constant_dynamic-update-slice_fusion.21
  549.4 3.0 convolution_subtract_fusion
  552.4 0.7 constant_dynamic-update-slice_fusion.20
  553.1 3.4 convolution_subtract_fusion.1
  556.5 0.7 constant_dynamic-update-slice_fusion.19
  557.2 3.7 convolution_subtract_fusion.4
  560.9 0.7 constant_dynamic-update-slice_fusion.18
  561.6 3.9 convolution_subtract_fusion.3
  565.5 0.7 convolution_dynamic-update-slice_fusion
  566.2 2.3 copy-done
  569.0 0.9 broadcast_select_fusion.2
  570.0 27.1 %all-gather.10.cloned.1.call-done = f32[4608,128]{1,0:T(8,128)} async-done(((f32[1152,128]{1,0:T(8,128)}), f32[4608,128]{1,0:T(8,128)}) %all-gather.10.cloned.1.call-update) | async-done | bytes 2359312 | tf_op jit(solution)/shard_map/all_gather | solution.py:9
  597.1 9.8 %conditional.8 = (f32[1152,128]{0,1:T(8,128)S(1)}) conditional(s32[]{:T(128)} %convert_element_type.45, (f32[1152,128]{1,0:T(8,128)S(1)}) %tuple.143, (f32[1152,4608]{1,0:T(8,128)}, f32[4,1152,128]{2,1,0:T(8,128)}, f32[1152,128]{1,0:T(8,128)S(1)}, f32[]{:T(128)}) %tuple.146), branch_computations={%region_3.4_spmd, %region_4.5_spmd} | conditional | flops 2039021568 | bytes 11206668 | solution.py:46
  597.3 1.9 reduce_sum.30
  599.1 7.8 %fusion.5 = f32[1152,128]{0,1:T(8,128)S(1)} fusion(f32[1152,128]{0,1:T(8,128)S(1)} %copy.11, f32[1152,128]{1,0:T(8,128)S(1)} %reduce_sum.30, f32[1152,4608]{1,0:T(8,128)} %get-tuple-element.83), kind=kOutput, calls=%fused_computation.5 | convolution fusion | flops 2038579200 | bytes 7077888 | tf_op jit(solution)/shard_map/cond/branch_1_fun/dot_general | solution.py:13
  607.0 0.9 broadcast_select_fusion.1
  607.9 30.3 %all-gather.12.cloned.1.call-done = f32[4608,128]{1,0:T(8,128)} async-done(((f32[1152,128]{1,0:T(8,128)}), f32[4608,128]{1,0:T(8,128)}) %all-gather.12.cloned.1.call-update) | async-done | bytes 2359312 | tf_op jit(solution)/shard_map/all_gather | solution.py:9
  638.2 10.0 %conditional.10 = (f32[1152,128]{0,1:T(8,128)S(1)}) conditional(s32[]{:T(128)} %convert_element_type.47, f32[1152,128]{0,1:T(8,128)S(1)} %get-tuple-element.217, (f32[1152,4608]{1,0:T(8,128)}, f32[4,1152,128]{2,1,0:T(8,128)}, f32[1152,128]{0,1:T(8,128)S(1)}, f32[]{:T(128)}) %tuple.147), branch_computations={%region_8.9_spmd, %region_9.10_spmd} | conditional | flops 2039021568 | bytes 10027020 | solution.py:46
  638.4 1.9 reduce_sum.31
  640.2 7.9 %fusion.13 = f32[1152,128]{0,1:T(8,128)S(1)} fusion(f32[1152,128]{0,1:T(8,128)S(1)} %get-tuple-element.73, f32[1152,128]{1,0:T(8,128)S(1)} %reduce_sum.31, f32[1152,4608]{1,0:T(8,128)} %get-tuple-element.86), kind=kOutput, calls=%fused_computation.9 | convolution fusion | flops 2038579200 | bytes 7077888 | tf_op jit(solution)/shard_map/cond/branch_1_fun/dot_general | solution.py:13
  648.3 0.9 broadcast_select_fusion
  650.0 29.6 %all-gather.14.cloned.1.call-done = f32[4608,128]{1,0:T(8,128)} async-done(((f32[1152,128]{1,0:T(8,128)}), f32[4608,128]{1,0:T(8,128)}) %all-gather.14.cloned.1.call-update) | async-done | bytes 2359312 | tf_op jit(solution)/shard_map/all_gather | solution.py:9
  679.6 10.0 %conditional.12 = (f32[1152,128]{0,1:T(8,128)S(1)}) conditional(s32[]{:T(128)} %convert_element_type.49, f32[1152,128]{0,1:T(8,128)S(1)} %get-tuple-element.219, (f32[4,1152,128]{2,1,0:T(8,128)}, f32[1152,4608]{1,0:T(8,128)}, f32[1152,128]{0,1:T(8,128)S(1)}) %tuple.145), branch_computations={%region_12.13_spmd, %region_13.15_spmd} | conditional | flops 2039021568 | bytes 10027020 | solution.py:46
  679.8 1.9 reduce_sum.25
  681.7 7.9 %fusion.21 = f32[1152,128]{0,1:T(8,128)S(1)} fusion(f32[1152,128]{0,1:T(8,128)S(1)} %get-tuple-element.78, f32[1152,128]{1,0:T(8,128)S(1)} %reduce_sum.25, f32[1152,4608]{1,0:T(8,128)} %get-tuple-element.80), kind=kOutput, calls=%fused_computation.13 | convolution fusion | flops 2038579200 | bytes 7077888 | tf_op jit(solution)/shard_map/cond/branch_1_fun/dot_general | solution.py:13
  689.6 7.6 %conditional.13 = (f32[1152,128]{0,1:T(8,128)S(1)}) conditional(s32[]{:T(128)} %convert_element_type.48, () %tuple.55, (f32[1152,1152]{1,0:T(8,128)}, f32[1152,128]{0,1:T(8,128)S(1)}) %tuple.141), branch_computations={%region_15.16_spmd, %region_16.17_spmd} | conditional | flops 2038431744 | bytes 6488072 | solution.py:34
  689.7 7.6 %fusion.64 = f32[1152,128]{0,1:T(8,128)S(1)} fusion(f32[1152,1152]{1,0:T(8,128)} %get-tuple-element.81, f32[1152,128]{0,1:T(8,128)S(1)} %get-tuple-element.116), kind=kOutput, calls=%fused_computation.125 | convolution fusion | flops 2038431744 | bytes 6488064 | tf_op jit(solution)/shard_map/cond | solution.py:34
  697.6 0.6 gather_fusion
  698.2 0.9 select_bitcast_fusion.1
  699.1 5.4 all-to-all-start
  704.5 9.8 %all-to-all-done = f32[8,2,8,1152]{3,2,1,0:T(8,128)S(1)} async-done(((f32[8,2,8,1152]{3,2,1,0:T(8,128)}), f32[8,2,8,1152]{3,2,1,0:T(8,128)S(1)}, u32[]{:S(2)}, u32[]{:S(2)}) %all-to-all-start) | async-done | bytes 589856 | tf_op jit(solution)/shard_map/all_to_all | solution.py:56
  714.9 1.2 gather_fusion.1
  716.4 0.9 copy.22
  (51 shorter events, 4.7 us)
Async XLA Ops:
  6.5 410.0 %all-gather.8.cloned.1.call-start = ((), (), s32[]{:S(2)}) async-start(), calls=%async_computation.1 | async-start | bytes 23887872 | tf_op jit(solution)/shard_map/all_gather | solution.py:19
  7.3 589.8 %all-gather.10.cloned.1.call-start = ((), (), s32[]{:S(2)}) async-start(), calls=%async_computation.2 | async-start | bytes 2949120 | tf_op jit(solution)/shard_map/all_gather | solution.py:9
  536.8 3.6 copy-start.1
  560.9 5.3 copy-start.2
  566.2 2.3 copy-start
  569.9 68.3 %all-gather.12.cloned.1.call-start = ((), (), s32[]{:S(2)}) async-start(), calls=%async_computation.3 | async-start | bytes 2949120 | tf_op jit(solution)/shard_map/all_gather | solution.py:9
  607.9 71.8 %all-gather.14.cloned.1.call-start = ((), (), s32[]{:S(2)}) async-start(), calls=%async_computation.4 | async-start | bytes 2949120 | tf_op jit(solution)/shard_map/all_gather | solution.py:9
  648.2 1.0 copy-start.3
  648.2 1.1 copy-start.4
  699.1 15.3 %all-to-all-start = ((f32[8,2,8,1152]{3,2,1,0:T(8,128)}), f32[8,2,8,1152]{3,2,1,0:T(8,128)S(1)}, u32[]{:S(2)}, u32[]{:S(2)}) async-start(f32[8,2,8,1152]{3,2,1,0:T(8,128)} %select_bitcast_fusion.1), calls=%async_computation | async-start | bytes 1179648 | tf_op jit(solution)/shard_map/all_to_all | solution.py:56
Sparse Core Ops, SparseCore 0:
  8.9 407.6 all-gather.7
  570.0 26.9 all-gather.9
  608.0 30.1 all-gather.11
  649.3 30.3 all-gather.13
